TPU v7x, 32 devices: a whole 2x2x4 slice. The times are simulated.
32 devices in a mesh: gx: 8 (over y, x, core), gy: 4 (over z).
Axes of the slice: x: 2, y: 2, z: 4, core: 2. Of those that a mesh axis runs over, the one named last changes fastest.
Arguments:
- collocation: bfloat16 [3072, 16384], P(None, 'gx'), may hold values from -6 to 6
- density: bfloat16 [3072, 3072], P('gy'), may hold values from -0.109375 to 0.109375
- kernel: bfloat16 [16384, 8, 4, 512], P('gx', None, 'gy'), may hold values from -6.67572e-06 to 6.67572e-06
Outputs:
- exchange: float32 [3072, 3072], P('gx', 'gy')
All inputs are finite; a program needn't handle non-finite values.
Results may differ from a plain program's by a relative error of at most 0.008.
Values may be sent and summed in bfloat16 or wider, within the bound.
A program may use at most 448 MiB of HBM per device.

v0:
```python
import jax
import jax.numpy as jnp
from jax import lax
from jax.sharding import PartitionSpec as P


def local(collocation, density, kernel):
    piece_width = kernel.shape[3]
    column_group = lax.axis_index("gy")
    own_rows = jnp.dot(density, collocation, preferred_element_type=jnp.float32).astype(
        jnp.bfloat16
    )
    dense_block = lax.all_gather(own_rows, "gy", axis=0, tiled=True)
    own_piece = lax.dynamic_slice_in_dim(collocation, column_group * piece_width, piece_width, 1)
    kernel_tiles = kernel[:, :, 0, :]
    panel_rows = kernel_tiles.shape[0]
    gathered = lax.all_gather(own_piece, "gx", axis=1, tiled=True)
    products = lax.dot_general(
        dense_block, gathered, (((0,), (0,)), ((), ())), preferred_element_type=jnp.float32
    )
    coefficients = kernel_tiles.reshape(panel_rows, gathered.shape[1])
    weighted = (coefficients.astype(jnp.float32) * products).astype(jnp.bfloat16)
    chosen = gathered
    reduced_cols = lax.psum_scatter(
        lax.dot_general(
            chosen, weighted, (((1,), (1,)), ((), ())), preferred_element_type=jnp.float32
        ),
        "gy",
        scatter_dimension=0,
        tiled=True,
    ).astype(jnp.bfloat16)
    chosen = collocation
    return lax.psum_scatter(
        lax.dot_general(
            chosen, reduced_cols, (((1,), (1,)), ((), ())), preferred_element_type=jnp.float32
        ),
        "gx",
        scatter_dimension=0,
        tiled=True,
    )


def solution(mesh):
    return jax.shard_map(
        local,
        mesh=mesh,
        in_specs=(P(None, "gx"), P("gy", None), P("gx", None, "gy", None)),
        out_specs=P("gx", "gy"),
        check_vma=False,
    )
```

profile of v0, /device:TPU:0, one launch (start us, length us, event | category | flops | bytes accessed | tf_op | source)
XLA Modules:
  0.0 1016.0 jit_solution(8901126047309515792)
XLA Ops:
  6.5 0.0 all-gather.5.cloned.1.call-start
  6.5 15.4 %convolution_convert_fusion = bf16[768,2048]{1,0:T(8,128)(2,1)} fusion(bf16[768,3072]{1,0:T(8,128)(2,1)} %param.4, bf16[3072,2048]{1,0:T(8,128)(2,1)} %param.3), kind=kOutput, calls=%fused_computation.2 | convolution fusion | flops 9665249280 | bytes 20447232 | tf_op jit(solution)/shard_map/dot_general | solution.py:10
  22.0 0.0 all-gather.5.cloned.1.call-update
  22.0 0.0 all-gather.3.cloned.1.call-start
  22.0 3.8 constant_dynamic-slice_fusion
  25.8 0.0 all-gather.3.cloned.1.call-update
  25.9 0.0 reduce-scatter.3.cloned.1.call-start
  25.9 20.2 %copy.5 = f32[256,8,8,512]{3,1,2,0:T(8,128)} copy(bf16[256,8,8,512]{3,2,1,0:T(8,128)(2,1)} %bitcast.15) | data formatting | bytes 50331648
  46.1 197.0 %all-gather.5.cloned.1.call-done = bf16[3072,2048]{1,0:T(8,128)(2,1)} async-done(((bf16[768,2048]{1,0:T(8,128)(2,1)}), bf16[3072,2048]{1,0:T(8,128)(2,1)}) %all-gather.5.cloned.1.call-update) | async-done | bytes 12582928 | tf_op jit(solution)/shard_map/all_gather | solution.py:13
  243.1 130.3 %all-gather.3.cloned.1.call-done = bf16[3072,4096]{1,0:T(8,128)(2,1)} async-done(((bf16[3072,512]{1,0:T(8,128)(2,1)}), bf16[3072,4096]{1,0:T(8,128)(2,1)}) %all-gather.3.cloned.1.call-update) | async-done | bytes 25165840 | tf_op jit(solution)/shard_map/all_gather | solution.py:17
  373.3 62.4 %multiply_convert_fusion = bf16[2048,4096]{1,0:T(8,128)(2,1)} fusion(f32[2048,4096]{1,0:T(8,128)} %bitcast.14, bf16[3072,2048]{1,0:T(8,128)(2,1)} %all-gather.5.cloned.1.call-done, bf16[3072,4096]{1,0:T(8,128)(2,1)} %all-gather.3.cloned.1.call-done), kind=kOutput, calls=%fused_computation | convolution fusion | flops 51556384768 | bytes 88080384 | tf_op jit(solution)/shard_map/dot_general | solution.py:18
  435.7 61.0 %fusion.1 = f32[3072,2048]{1,0:T(8,128)} fusion(bf16[3072,4096]{1,0:T(8,128)(2,1)} %all-gather.3.cloned.1.call-done, bf16[2048,4096]{1,0:T(8,128)(2,1)} %multiply_convert_fusion), kind=kOutput, calls=%fused_computation.5 | convolution fusion | flops 51539607552 | bytes 67108864 | tf_op jit(solution)/shard_map/dot_general | solution.py:25
  496.7 0.0 reduce-scatter.3.cloned.1.call-update
  496.8 0.0 reduce-scatter.5.cloned.1.call-start
  496.8 414.3 %reduce-scatter.3.cloned.1.call-done = f32[768,2048]{1,0:T(8,128)} async-done(((f32[3072,2048]{1,0:T(8,128)}), f32[768,2048]{1,0:T(8,128)}) %reduce-scatter.3.cloned.1.call-update) | async-done | bytes 6291472 | tf_op jit(solution)/shard_map/reduce_scatter | solution.py:24
  911.1 16.9 %convolution_bitcast_fusion = f32[3072,768]{0,1:T(8,128)} fusion(bf16[3072,2048]{1,0:T(8,128)(2,1)} %param.3, f32[768,2048]{1,0:T(8,128)} %reduce-scatter.3.cloned.1.call-done), kind=kOutput, calls=%fused_computation.1 | convolution fusion | flops 9665249280 | bytes 28311552 | tf_op jit(solution)/shard_map/dot_general | solution.py:34
  928.0 0.0 reduce-scatter.5.cloned.1.call-update
  928.1 78.8 %reduce-scatter.5.cloned.1.call-done = f32[384,768]{0,1:T(8,128)} async-done(((f32[3072,768]{0,1:T(8,128)}), f32[384,768]{0,1:T(8,128)}) %reduce-scatter.5.cloned.1.call-update) | async-done | bytes 1179664 | tf_op jit(solution)/shard_map/reduce_scatter | solution.py:33
  1006.8 2.7 copy.4
Async XLA Ops:
  6.5 236.5 %all-gather.5.cloned.1.call-start = ((), (), s32[]{:S(2)}) async-start(), calls=%async_computation.3 | async-start | bytes 15728640 | tf_op jit(solution)/shard_map/all_gather | solution.py:13
  22.0 351.3 %all-gather.3.cloned.1.call-start = ((), (), s32[]{:S(2)}) async-start(), calls=%async_computation.2 | async-start | bytes 28311552 | tf_op jit(solution)/shard_map/all_gather | solution.py:17
  25.9 885.3 %reduce-scatter.3.cloned.1.call-start = ((), (), s32[]{:S(2)}) async-start(), calls=%async_computation.4 | async-start | bytes 31457280 | tf_op jit(solution)/shard_map/reduce_scatter | solution.py:24
  496.8 510.0 %reduce-scatter.5.cloned.1.call-start = ((), (), s32[]{:S(2)}) async-start(), calls=%async_computation.5 | async-start | bytes 10616832 | tf_op jit(solution)/shard_map/reduce_scatter | solution.py:33
Sparse Core Ops, SparseCore 0:
  22.1 220.8 all-gather.4
  244.9 128.3 all-gather.2
  496.9 414.1 reduce-scatter.2
  928.2 78.5 reduce-scatter.4
where the time goes:
time: 1020 us
  waiting for transfers between devices  820 us (80%)
  matrix products  156 us (15%)
  local copies, waits for them, and re-layouts  26.6 us (3%)
  between operations  13.1 us (1%)
    reduce_scatter x1, waiting for transfers between devices, local(): lax.psum_scatter(lax.dot_general(chosen, weighted, (((1,), (1,)), ((), ()...  414 us
    all_gather x1, waiting for transfers between devices, local(): dense_block = lax.all_gather(own_rows, 'gy', axis=0, tiled=True)  197 us
    all_gather x1, waiting for transfers between devices, local(): gathered = lax.all_gather(own_piece, 'gx', axis=1, tiled=True)  130 us
    reduce_scatter x1, waiting for transfers between devices, local(): lax.psum_scatter(lax.dot_general(chosen, reduced_cols, (((1,), (1,)), (()...  78.8 us
    dot_general x1, matrix products, local(): lax.dot_general(dense_block, gathered, (((0,), (0,)), ((), ())), preferre...  62.4 us
    dot_general x1, matrix products, local(): lax.dot_general(chosen, weighted, (((1,), (1,)), ((), ())), preferred_ele...  61 us
  transfers between devices with their start and end apart: 4, of which 4 were waited for; matrix products, arithmetic and copies ran while one was open for 2% of the time, Pallas kernels for 0%

commit v1 on v0

--- a/solution.py
+++ b/solution.py
@@ -10,7 +10,12 @@
     own_rows = jnp.dot(density, collocation, preferred_element_type=jnp.float32).astype(
         jnp.bfloat16
     )
-    dense_block = lax.all_gather(own_rows, "gy", axis=0, tiled=True)
+    ring = [own_rows]
+    for hop in range(3):
+        ring.append(lax.ppermute(ring[-1], "gy", [(dev, (dev + 1) % 4) for dev in range(4)]))
+    dense_block = jnp.roll(
+        jnp.concatenate(ring[::-1], axis=0), (lax.axis_index("gy") + 1) * ring[0].shape[0], axis=0
+    )
     own_piece = lax.dynamic_slice_in_dim(collocation, column_group * piece_width, piece_width, 1)
     kernel_tiles = kernel[:, :, 0, :]
     panel_rows = kernel_tiles.shape[0]

time: 1020 us -> 909 us (0.89)
  waiting for transfers between devices: 820 us -> 683 us
  local copies, waits for them, and re-layouts: 26.6 us -> 53.8 us
    all_gather x1 -> x0, waiting for transfers between devices: 197 us -> none  [local(): dense_block = lax.all_gather(own_rows, 'gy', axis=0, tiled=True)]
    ppermute x0 -> x3, waiting for transfers between devices: none -> 192 us  [local(): lax.ppermute(ring[-1], 'gy', [(dev, (dev + 1) % 4) for dev in range(4)])]
    all_gather x1, waiting for transfers between devices: 130 us -> 0.01 us  [local(): gathered = lax.all_gather(own_piece, 'gx', axis=1, tiled=True)]
    unnamed x1 -> x12, local copies, waits for them, and re-layouts: 20.2 us -> 45.5 us
  transfers between devices with their start and end apart: 4 -> 6, of which waited for: 4 -> 5; matrix products, arithmetic and copies ran while one was open for 2% -> 7% of each run, Pallas kernels for 0% -> 0%
where the time goes in v1:
time: 909 us; the launch traced here: 908 us
  waiting for transfers between devices  683 us (75%)
  matrix products  155 us (17%)
  local copies, waits for them, and re-layouts  53.8 us (6%)
  between operations  13.1 us (1%)
    reduce_scatter x1, waiting for transfers between devices, local(): lax.psum_scatter(lax.dot_general(chosen, weighted, (((1,), (1,)), ((), ()...  412 us
    ppermute x3, waiting for transfers between devices, local(): lax.ppermute(ring[-1], 'gy', [(dev, (dev + 1) % 4) for dev in range(4)])  192 us
    reduce_scatter x1, waiting for transfers between devices, local(): lax.psum_scatter(lax.dot_general(chosen, reduced_cols, (((1,), (1,)), (()...  78.7 us
    dot_general x1, matrix products, local(): lax.dot_general(dense_block, gathered, (((0,), (0,)), ((), ())), preferre...  62.7 us
    dot_general x1, matrix products, local(): lax.dot_general(chosen, weighted, (((1,), (1,)), ((), ())), preferred_ele...  61 us
    unnamed x12, local copies, waits for them, and re-layouts  45.5 us
  transfers between devices with their start and end apart: 6, of which 5 were waited for; matrix products, arithmetic and copies ran while one was open for 7% of the time, Pallas kernels for 0%

profile of v1, /device:TPU:0, one launch (start us, length us, event | category | flops | bytes accessed | tf_op | source)
XLA Modules:
  0.0 908.1 jit_solution(16752154800002937877)
XLA Ops:
  6.5 0.0 all-gather.2.cloned.1.call-start
  6.5 3.8 constant_dynamic-slice_fusion
  10.3 0.0 all-gather.2.cloned.1.call-update
  10.3 0.0 reduce-scatter.3.cloned.1.call-start
  10.4 14.3 %convolution_convert_fusion = bf16[768,2048]{1,0:T(8,128)(2,1)S(1)} fusion(bf16[768,3072]{1,0:T(8,128)(2,1)} %param.4, bf16[3072,2048]{1,0:T(8,128)(2,1)} %param.3), kind=kOutput, calls=%fused_computation.3 | convolution fusion | flops 9665249280 | bytes 20447232 | tf_op jit(solution)/shard_map/dot_general | solution.py:10
  24.6 3.1 collective-permute-start
  27.7 70.1 %collective-permute-done = bf16[768,2048]{1,0:T(8,128)(2,1)S(1)} collective-permute-done((bf16[768,2048]{1,0:T(8,128)(2,1)S(1)}, bf16[768,2048]{1,0:T(8,128)(2,1)S(1)}, u32[]{:S(2)}, u32[]{:S(2)}) %collective-permute-start) | collective-permute-done | bytes 3145760 | tf_op jit(solution)/shard_map/ppermute | solution.py:15
  97.9 0.0 copy-start
  97.9 1.7 copy-done
  99.6 0.0 collective-permute-start.1
  99.6 71.2 %collective-permute-done.1 = bf16[768,2048]{1,0:T(8,128)(2,1)} collective-permute-done((bf16[768,2048]{1,0:T(8,128)(2,1)S(1)}, bf16[768,2048]{1,0:T(8,128)(2,1)}, u32[]{:S(2)}, u32[]{:S(2)}) %collective-permute-start.1) | collective-permute-done | bytes 3145760 | tf_op jit(solution)/shard_map/ppermute | solution.py:15
  170.8 0.0 collective-permute-start.2
  170.8 19.6 %copy.5 = f32[256,8,8,512]{3,1,2,0:T(8,128)} copy(bf16[256,8,8,512]{3,2,1,0:T(8,128)(2,1)} %bitcast.15) | data formatting | bytes 50331648
  190.4 50.9 %collective-permute-done.2 = bf16[768,2048]{1,0:T(8,128)(2,1)} collective-permute-done((bf16[768,2048]{1,0:T(8,128)(2,1)}, bf16[768,2048]{1,0:T(8,128)(2,1)}, u32[]{:S(2)}, u32[]{:S(2)}) %collective-permute-start.2) | collective-permute-done | bytes 3145760 | tf_op jit(solution)/shard_map/ppermute | solution.py:15
  241.3 4.0 constant_dynamic-update-slice_fusion.7
  245.3 0.0 copy-start.1
  245.3 4.2 constant_dynamic-update-slice_fusion.6
  249.4 3.9 constant_dynamic-update-slice_fusion.5
  253.4 1.9 constant_dynamic-update-slice_fusion.4
  255.3 3.9 constant_dynamic-update-slice_fusion.3
  259.2 4.0 constant_dynamic-update-slice_fusion.2
  263.2 0.0 copy-done.1
  263.2 2.2 constant_dynamic-update-slice_fusion.1
  265.4 1.9 constant_dynamic-update-slice_fusion
  267.3 0.0 all-gather.2.cloned.1.call-done
  267.3 62.7 %multiply_convert_fusion = bf16[2048,4096]{1,0:T(8,128)(2,1)} fusion(f32[2048,4096]{1,0:T(8,128)} %bitcast.14, bf16[3072,4096]{1,0:T(8,128)(2,1)} %all-gather.2.cloned.1.call-done, bf16[6144,2048]{1,0:T(8,128)(2,1)} %constant_dynamic-update-slice_fusion, s32[]{:T(128)S(6)} %select_n.18), kind=kOutput, calls=%fused_computation | convolution fusion | flops 51556384768 | bytes 88080384 | tf_op jit(solution)/shard_map/dot_general | solution.py:23
  330.1 61.0 %fusion.3 = f32[3072,2048]{1,0:T(8,128)} fusion(bf16[3072,4096]{1,0:T(8,128)(2,1)} %all-gather.2.cloned.1.call-done, bf16[2048,4096]{1,0:T(8,128)(2,1)} %multiply_convert_fusion), kind=kOutput, calls=%fused_computation.15 | convolution fusion | flops 51539607552 | bytes 67108864 | tf_op jit(solution)/shard_map/dot_general | solution.py:30
  391.0 0.0 reduce-scatter.3.cloned.1.call-update
  391.0 0.0 reduce-scatter.5.cloned.1.call-start
  391.1 412.1 %reduce-scatter.3.cloned.1.call-done = f32[768,2048]{1,0:T(8,128)} async-done(((f32[3072,2048]{1,0:T(8,128)}), f32[768,2048]{1,0:T(8,128)}) %reduce-scatter.3.cloned.1.call-update) | async-done | bytes 6291472 | tf_op jit(solution)/shard_map/reduce_scatter | solution.py:29
  803.2 17.0 %convolution_bitcast_fusion = f32[3072,768]{0,1:T(8,128)} fusion(bf16[3072,2048]{1,0:T(8,128)(2,1)} %param.3, f32[768,2048]{1,0:T(8,128)} %reduce-scatter.3.cloned.1.call-done), kind=kOutput, calls=%fused_computation.2 | convolution fusion | flops 9665249280 | bytes 28311552 | tf_op jit(solution)/shard_map/dot_general | solution.py:39
  820.2 0.0 reduce-scatter.5.cloned.1.call-update
  820.2 78.7 %reduce-scatter.5.cloned.1.call-done = f32[384,768]{0,1:T(8,128)} async-done(((f32[3072,768]{0,1:T(8,128)}), f32[384,768]{0,1:T(8,128)}) %reduce-scatter.5.cloned.1.call-update) | async-done | bytes 1179664 | tf_op jit(solution)/shard_map/reduce_scatter | solution.py:38
  898.9 2.7 copy.4
Async XLA Ops:
  6.5 260.8 %all-gather.2.cloned.1.call-start = ((), (), s32[]{:S(2)}) async-start(), calls=%async_computation.2 | async-start | bytes 28311552 | tf_op jit(solution)/shard_map/all_gather | solution.py:22
  10.3 792.9 %reduce-scatter.3.cloned.1.call-start = ((), (), s32[]{:S(2)}) async-start(), calls=%async_computation.3 | async-start | bytes 31457280 | tf_op jit(solution)/shard_map/reduce_scatter | solution.py:29
  24.6 73.2 %collective-permute-start = (bf16[768,2048]{1,0:T(8,128)(2,1)S(1)}, bf16[768,2048]{1,0:T(8,128)(2,1)S(1)}, u32[]{:S(2)}, u32[]{:S(2)}) collective-permute-start(bf16[768,2048]{1,0:T(8,128)(2,1)S(1)} %convolution_convert_fusion), channel_id=1, source_target_pairs={{0,1},{1,2},{2,3},{3,0},{4,5},{5,6},{6,7},{7,4},{8,9},{9,10},{10,1... | collective-permute-start | bytes 9437192 | tf_op jit(solution)/shard_map/ppermute | solution.py:15
  97.9 1.7 copy-start
  99.6 71.2 %collective-permute-start.1 = (bf16[768,2048]{1,0:T(8,128)(2,1)S(1)}, bf16[768,2048]{1,0:T(8,128)(2,1)}, u32[]{:S(2)}, u32[]{:S(2)}) collective-permute-start(bf16[768,2048]{1,0:T(8,128)(2,1)S(1)} %collective-permute-done), channel_id=1, source_target_pairs={{0,1},{1,2},{2,3},{3,0},{4,5},{5,6},{6,7},{7,4},{8,9},{9,10},{10,1... | collective-permute-start | bytes 9437192 | tf_op jit(solution)/shard_map/ppermute | solution.py:15
  170.8 70.5 %collective-permute-start.2 = (bf16[768,2048]{1,0:T(8,128)(2,1)}, bf16[768,2048]{1,0:T(8,128)(2,1)}, u32[]{:S(2)}, u32[]{:S(2)}) collective-permute-start(bf16[768,2048]{1,0:T(8,128)(2,1)} %collective-permute-done.1), channel_id=1, source_target_pairs={{0,1},{1,2},{2,3},{3,0},{4,5},{5,6},{6,7},{7,4},{8,9},{9,10},{10,1... | collective-permute-start | bytes 9437192 | tf_op jit(solution)/shard_map/ppermute | solution.py:15
  245.3 17.9 %copy-start.1 = (bf16[768,2048]{1,0:T(8,128)(2,1)S(1)}, bf16[768,2048]{1,0:T(8,128)(2,1)}, u32[]{:S(2)}) copy-start(bf16[768,2048]{1,0:T(8,128)(2,1)} %copy-done) | copy-start | bytes 9437188
  391.0 507.9 %reduce-scatter.5.cloned.1.call-start = ((), (), s32[]{:S(2)}) async-start(), calls=%async_computation.4 | async-start | bytes 10616832 | tf_op jit(solution)/shard_map/reduce_scatter | solution.py:38
Sparse Core Ops, SparseCore 0:
  10.4 132.8 all-gather.1
  391.2 411.9 reduce-scatter.2
  820.3 78.5 reduce-scatter.4
